TPU v7x, 32 devices: a whole 2x2x4 slice. The times are simulated.
32 devices in a mesh: node: 32 (over z, y, x, core).
Axes of the slice: x: 2, y: 2, z: 4, core: 2. Of those that a mesh axis runs over, the one named last changes fastest.
Arguments:
- params: float32 [16384, 2048], P('node'), may hold values from -6 to 6
- public: float32 [16384, 2048], P('node'), may hold values from -4 to 4
- peer_public: float32 [16384, 2048], P('node'), may hold values from -8 to 8
- round_index: int32 [1], replicated, may hold values from 0 to 63
Outputs:
- params_new: float32 [16384, 2048], P('node')
- public_new: float32 [16384, 2048], P('node')
- peer_public_new: float32 [16384, 2048], P('node')
- consensus_gap: float32 [], replicated
All inputs are finite; a program needn't handle non-finite values.
Results may differ from a plain program's by a relative error of at most 0.0003.
Values may be sent and summed in bfloat16 or wider, within the bound.
A program may use at most 128 MiB of HBM per device.

v0:
```python
from functools import partial

import jax
import jax.numpy as jnp
from jax import lax
from jax.experimental import pallas as pl
from jax.experimental.pallas import tpu as pltpu
from jax.sharding import PartitionSpec as P

BLOCK = 128
MIX = 0.4
WIDE = 512
STRIP = 128

def swap_kernel(
    bit,
    inverse,
    params_hbm,
    public_hbm,
    peer_hbm,
    params_out,
    public_out,
    peer_out,
    gap_out,
    params_in,
    public_in,
    peer_in,
    coded,
    scale,
    got_coded,
    got_scale,
    load_sem,
    peer_sem,
    send_sem,
    recv_sem,
    part,
    rows_in,
    part_send_sem,
    part_recv_sem,
):
    chunks = coded.shape[0]
    across = params_hbm.shape[1] // WIDE
    me = lax.axis_index("node")
    mask = 1 << bit
    other = me + mask - 2 * mask * (me // mask % 2)

    barrier = pltpu.get_barrier_semaphore()
    n = rows_in.shape[0]

    def greet(k, carry):
        pl.semaphore_signal(
            barrier, inc=1, device_id=(lax.rem(me + k, n),), device_id_type=pl.DeviceIdType.MESH
        )
        return carry

    lax.fori_loop(1, n, greet, 0)

    def place(k):
        rows = pl.ds(pl.multiple_of(k // across * BLOCK, BLOCK), BLOCK)
        return rows, pl.multiple_of(k % across * WIDE, WIDE)

    def load(k, source, target, sem):
        rows, first = place(k)
        here = (rows, pl.ds(first, WIDE))
        return pltpu.make_async_copy(source.at[here], target.at[here], sem)

    def send(k, part):
        source, target = ((coded, got_coded), (scale, got_scale))[part]
        return pltpu.make_async_remote_copy(
            src_ref=source.at[k],
            dst_ref=target.at[k],
            send_sem=send_sem.at[part, k],
            recv_sem=recv_sem.at[part, k],
            device_id=(other,),
            device_id_type=pl.DeviceIdType.MESH,
        )

    def begin(k, carry):
        load(k, params_hbm, params_in, load_sem.at[0, k]).start()
        load(k, public_hbm, public_in, load_sem.at[1, k]).start()
        return carry

    lax.fori_loop(0, chunks, begin, 0)

    def begin_peer(k, carry):
        load(k, peer_hbm, peer_in, peer_sem.at[k]).start()
        return carry

    lax.fori_loop(0, chunks, begin_peer, 0)

    def encode(k, carry):
        rows, first = place(k)
        load(k, params_hbm, params_in, load_sem.at[0, k]).wait()
        load(k, public_hbm, public_in, load_sem.at[1, k]).wait()
        for strip in range(0, WIDE, STRIP):
            columns = pl.ds(pl.multiple_of(first + strip, STRIP), STRIP)
            difference = params_in[rows, columns] - public_in[rows, columns]
            peak = jnp.max(jnp.abs(difference), axis=0, keepdims=True) + 1e-06
            rounded = peak.astype(jnp.bfloat16)
            scale[k, :, strip : strip + STRIP] = rounded
            wide = rounded.astype(jnp.float32)
            level = jnp.floor(difference / wide * 127.0 + 0.5)
            coded[k, :, strip : strip + STRIP] = level.astype(jnp.bfloat16)
        for strip in range(0, WIDE, STRIP):
            columns = pl.ds(pl.multiple_of(first + strip, STRIP), STRIP)
            factor = scale[k, :, strip : strip + STRIP].astype(jnp.float32) * (1.0 / 127.0)
            level = coded[k, :, strip : strip + STRIP].astype(jnp.float32)
            public_out[rows, columns] = public_in[rows, columns] + level * factor

        @pl.when(k == 0)
        def _():
            pl.semaphore_wait(barrier, n - 1)

        send(k, 1).start()
        send(k, 0).start()
        return carry

    lax.fori_loop(0, chunks, encode, 0)

    def combine(k, total):
        rows, first = place(k)
        load(k, peer_hbm, peer_in, peer_sem.at[k]).wait()
        send(k, 1).wait_recv()
        send(k, 0).wait_recv()
        for strip in range(0, WIDE, STRIP):
            columns = pl.ds(pl.multiple_of(first + strip, STRIP), STRIP)
            factor = got_scale[k, :, strip : strip + STRIP].astype(jnp.float32) * (1.0 / 127.0)
            level = got_coded[k, :, strip : strip + STRIP].astype(jnp.float32)
            peer_new = peer_in[rows, columns] + level * factor
            public_new = public_out[rows, columns]
            params_new = params_in[rows, columns] + MIX * (peer_new - public_new)
            peer_out[rows, columns] = peer_new
            params_out[rows, columns] = params_new
            distance = params_new - public_new
            total = total + jnp.sum(distance * distance, axis=0, keepdims=True)
        return total

    part[...] = lax.fori_loop(0, chunks, combine, jnp.zeros((1, STRIP), jnp.float32))

    def drain(k, carry):
        send(k, 1).wait_send()
        send(k, 0).wait_send()
        return carry

    lax.fori_loop(0, chunks, drain, 0)

    def row_copy(k, owner, target):
        return pltpu.make_async_remote_copy(
            src_ref=part,
            dst_ref=rows_in.at[owner],
            send_sem=part_send_sem.at[k],
            recv_sem=part_recv_sem.at[owner],
            device_id=(target,),
            device_id_type=pl.DeviceIdType.MESH,
        )

    def send_row(k, carry):
        row_copy(k, me, lax.rem(me + k, n)).start()
        return carry

    lax.fori_loop(1, n, send_row, 0)
    rows_in[me] = part[...]

    def take_row(k, carry):
        source = lax.rem(me + k, n)
        row_copy(k, source, source).wait()
        return carry

    lax.fori_loop(1, n, take_row, 0)
    summed = jnp.sum(rows_in[...], axis=0)
    gap_out[...] = jnp.broadcast_to(jnp.sum(summed, axis=1, keepdims=True) * inverse, gap_out.shape)


def store_kernel(*refs):
    sources, targets, sem = refs[:3], refs[3:6], refs[6]
    copies = [pltpu.make_async_copy(a, b, sem.at[i]) for i, (a, b) in enumerate(zip(sources, targets))]
    for copy in copies:
        copy.start()
    for copy in copies:
        copy.wait()


def store(*arrays):
    full = jax.ShapeDtypeStruct(arrays[0].shape, arrays[0].dtype)
    return pl.pallas_call(
        store_kernel,
        in_specs=[pl.BlockSpec(memory_space=pltpu.VMEM)] * 3,
        out_specs=[pl.BlockSpec(memory_space=pl.ANY)] * 3,
        out_shape=[full] * 3,
        scratch_shapes=[pltpu.SemaphoreType.DMA((3,))],
        compiler_params=pltpu.CompilerParams(vmem_limit_bytes=1 << 20),
    )(*arrays)


def round_of(bit, params, public, peer_public):
    *results, acc = swap(bit, params, public, peer_public)
    return (*store(*results), acc)


def swap(bit, params, public, peer_public):
    row_count, col_count = params.shape
    chunks = row_count // BLOCK * (col_count // WIDE)
    n = lax.axis_size("node")
    inverse = 1.0 / (n * row_count * col_count)
    full = pltpu.VMEM(params.shape, jnp.float32)
    vmem = pl.BlockSpec(memory_space=pltpu.VMEM)
    return pl.pallas_call(
        partial(swap_kernel, bit, inverse),
        in_specs=[pl.BlockSpec(memory_space=pl.ANY)] * 3,
        out_specs=[vmem] * 4,
        out_shape=[full, full, full, jax.ShapeDtypeStruct((1, STRIP), jnp.float32)],
        scratch_shapes=[
            pltpu.VMEM(params.shape, jnp.float32),
            pltpu.VMEM(params.shape, jnp.float32),
            pltpu.VMEM(params.shape, jnp.float32),
            pltpu.VMEM((chunks, BLOCK, WIDE), jnp.bfloat16),
            pltpu.VMEM((chunks, 1, WIDE), jnp.bfloat16),
            pltpu.VMEM((chunks, BLOCK, WIDE), jnp.bfloat16),
            pltpu.VMEM((chunks, 1, WIDE), jnp.bfloat16),
            pltpu.SemaphoreType.DMA((2, chunks)),
            pltpu.SemaphoreType.DMA((chunks,)),
            pltpu.SemaphoreType.DMA((2, chunks)),
            pltpu.SemaphoreType.DMA((2, chunks)),
            pltpu.VMEM((1, STRIP), jnp.float32),
            pltpu.VMEM((n, 1, STRIP), jnp.float32),
            pltpu.SemaphoreType.DMA((n,)),
            pltpu.SemaphoreType.DMA((n,)),
        ],
        cost_estimate=pl.CostEstimate(
            flops=30 * row_count * col_count,
            bytes_accessed=170 * row_count * col_count,
            transcendentals=0,
        ),
        compiler_params=pltpu.CompilerParams(
            collective_id=bit + 1, has_side_effects=True, vmem_limit_bytes=40 << 20
        ),
    )(params, public, peer_public)


def shards(params, public, peer_public, round_index):
    n = lax.axis_size("node")
    bit_count = n.bit_length() - 1
    chosen_bit = round_index[0] % bit_count
    branches = [partial(round_of, bit) for bit in range(bit_count)]
    params_new, public_new, peer_new, gap = lax.switch(
        chosen_bit, branches, params, public, peer_public
    )
    return (params_new, public_new, peer_new, gap[0, 0])


def solution(mesh):
    in_specs = (P("node", None), P("node", None), P("node", None), P())
    out_specs = (P("node", None), P("node", None), P("node", None), P())
    return jax.shard_map(shards, mesh=mesh, in_specs=in_specs, out_specs=out_specs, check_vma=False)
```

profile of v0, /device:TPU:0, one launch (start us, length us, event | category | flops | bytes accessed | tf_op | source)
XLA Modules:
  0.0 66.8 jit_solution(8481922003683303857)
XLA Ops:
  1.3 64.4 %conditional.1 = (f32[512,2048]{1,0:T(8,128)}, f32[512,2048]{1,0:T(8,128)}, f32[512,2048]{1,0:T(8,128)}, f32[1,128]{1,0:T(1,128)S(1)}) conditional(s32[]{:T(128)} %clamp.3, (f32[512,2048]{1,0:T(8,128)}, f32[512,2048]{1,0:T(8,128)}, f32[512,2048]{1,0:T(8,128)}) %tuple.28, (f32[512,2048]{1,0:T(8,128)}, ...), branch_computations={%region_0.1_spmd, %region_1.2_spmd, %region_2.3_spmd, %region_3.4_... | conditional | flops 31457280 | bytes 178257952 | solution.py:245
  1.3 59.6 %branch_3_fun.2 = (f32[512,2048]{1,0:T(8,128)S(1)}, f32[512,2048]{1,0:T(8,128)S(1)}, f32[512,2048]{1,0:T(8,128)S(1)}, f32[1,128]{1,0:T(1,128)S(1)}) custom-call(f32[512,2048]{1,0:T(8,128)} %get-tuple-element.60.params_hbm, f32[512,2048]{1,0:T(8,128)} %get-tuple-element.61.public_hbm, f32[512,2048]{1,0:T(8,128)} %get-tuple-element.62.peer_hbm), custom_call_target="tpu_custom_call" | custom-call | flops 31457280 | bytes 178257920 | tf_op jit(solution)/shard_map/cond/branch_3_fun/pallas_call | solution.py:207
  61.0 4.7 %branch_3_fun.3 = (f32[512,2048]{1,0:T(8,128)}, f32[512,2048]{1,0:T(8,128)}, f32[512,2048]{1,0:T(8,128)}) custom-call(f32[512,2048]{1,0:T(8,128)S(1)} %get-tuple-element.63.refs_0_, f32[512,2048]{1,0:T(8,128)S(1)} %get-tuple-element.64.refs_1_, f32[512,2048]{1,0:T(8,128)S(1)} %get-tuple-element.65.refs_2_), custom_call_target="tpu_custom_call" | custom-call | tf_op jit(solution)/shard_map/cond/branch_3_fun/pallas_call | solution.py:185
where the time goes:
time: 67.1 us; the launch traced here: 66.8 us
  Pallas kernels  64.3 us (96%)
  between operations  2.46 us (4%)
    pallas_call x1, Pallas kernels, swap(): pl.pallas_call(partial(swap_kernel, bit, inverse), in_specs=[pl.BlockSpec...  59.6 us
    pallas_call x1, Pallas kernels, store(): pl.pallas_call(store_kernel, in_specs=[pl.BlockSpec(memory_space=pltpu.VM...  4.68 us

commit v1 on v0

v1 whole, which is shorter than its diff:
```python
from functools import partial

import jax
import jax.numpy as jnp
from jax import lax
from jax.experimental import pallas as pl
from jax.experimental.pallas import tpu as pltpu
from jax.sharding import PartitionSpec as P

BLOCK = 128
MIX = 0.4
WIDE = 512
STRIP = 128
FIRST = (8, 16)
MESH = pl.DeviceIdType.MESH
ANY = pl.BlockSpec(memory_space=pl.ANY)
VMEM = pl.BlockSpec(memory_space=pltpu.VMEM)
HBM = pl.BlockSpec(memory_space=pltpu.HBM)


def place(k, col_count):
    across = col_count // WIDE
    rows = pl.ds(pl.multiple_of(k // across * BLOCK, BLOCK), BLOCK)
    return rows, pl.multiple_of(k % across * WIDE, WIDE)


def area(k, col_count):
    rows, first = place(k, col_count)
    return rows, pl.ds(first, WIDE)


def cut(chunks):
    first, second = (chunks * f // 16 for f in FIRST)
    return first + (second - first) * lax.rem(lax.axis_index("node"), 2)


class Pair:
    def __init__(self, bit, send_sem, recv_sem):
        self.me = lax.axis_index("node")
        self.mask = 1 << bit
        self.upper = self.me // self.mask % 2
        self.other = self.me + self.mask - 2 * self.mask * self.upper
        self.send_sem, self.recv_sem = send_sem, recv_sem

    def tell(self, sem):
        pl.semaphore_signal(sem, inc=1, device_id=(self.other,), device_id_type=MESH)

    def copy(self, source, target, part, k):
        return pltpu.make_async_remote_copy(
            src_ref=source,
            dst_ref=target,
            send_sem=self.send_sem.at[part, k],
            recv_sem=self.recv_sem.at[part, k],
            device_id=(self.other,),
            device_id_type=MESH,
        )


def merge(pair, k, slot, total, got_coded, got_scale, mine, shared, peer, mine_new, peer_new, spot):
    rows, first = place(k, shared.shape[1])
    for strip in range(0, WIDE, STRIP):
        columns = pl.ds(pl.multiple_of(first + strip, STRIP), STRIP)
        factor = got_scale[k, :, strip : strip + STRIP].astype(jnp.float32) * (1.0 / 127.0)
        level = got_coded[slot, :, strip : strip + STRIP].astype(jnp.float32)
        theirs = peer[rows, columns] + level * factor
        public_new = shared[rows, columns]
        params_new = mine[rows, columns] + MIX * (theirs - public_new)
        target = spot(rows, columns, strip)
        peer_new[target] = theirs
        mine_new[target] = params_new
        distance = params_new - public_new
        total = total + jnp.sum(distance * distance, axis=0, keepdims=True)
    return total


def greet_pairs(pair, n, barrier):
    half, mask = n // 2, pair.mask
    mine = pair.me // (2 * mask) * mask + pair.me % mask

    @pl.when(pair.upper == 0)
    def _():
        def greet(k, carry):
            t = lax.rem(mine + k, half)
            low = t // mask * (2 * mask) + t % mask
            pl.semaphore_signal(barrier, inc=1, device_id=(low,), device_id_type=MESH)
            return carry

        lax.fori_loop(1, half, greet, 0)


def hear_pairs(pair, n, barrier, all_in):
    @pl.when(pair.upper == 0)
    def _():
        pl.semaphore_wait(barrier, n // 2 - 1)
        pair.tell(all_in)


def add_rows(pair, part, rows_in, row_send, row_recv, all_in):
    n = rows_in.shape[0]

    @pl.when(pair.upper == 1)
    def _():
        pl.semaphore_wait(all_in, 1)

    def row_copy(source, place, target):
        return pltpu.make_async_remote_copy(
            src_ref=source,
            dst_ref=place,
            send_sem=row_send,
            recv_sem=row_recv,
            device_id=(target,),
            device_id_type=MESH,
        )

    def send_row(k, carry):
        row_copy(part, rows_in.at[pair.me], lax.rem(pair.me + k, n)).start()
        return carry

    lax.fori_loop(1, n, send_row, 0)
    rows_in[pair.me] = part[...]
    rest = rows_in.at[pl.ds(1, n - 1)]
    row_copy(rest, rest, pair.other).wait()
    return jnp.sum(jnp.sum(rows_in[...], axis=0), axis=1, keepdims=True)


def first_kernel(bit, lead, last, inverse, params_hbm, public_hbm, peer_hbm, *refs):
    mine, shared, peer = refs[:3]
    if last:
        gap_out, coded, got_coded, got_scale = refs[3:7]
        scale, load_sem, peer_sem, send_sem, recv_sem = refs[7:12]
        ready, all_in, part, rows_in, row_send, row_recv = refs[12:]
    else:
        coded, scale_out, part, got_coded, got_scale = refs[3:8]
        scale, load_sem, peer_sem, send_sem, recv_sem = refs[8:]
    chunks = coded.shape[0]
    cols = shared.shape[1]
    stop = chunks if last else cut(chunks)
    pair = Pair(bit, send_sem, recv_sem)
    barrier = pltpu.get_barrier_semaphore()

    if last:

        @pl.when(pair.upper == 0)
        def _():
            pair.tell(barrier)
    else:
        pair.tell(barrier)

    def load(k, source, target, sem):
        here = area(k, cols)
        return pltpu.make_async_copy(source.at[here], target.at[here], sem)

    def send_coded(k):
        return pair.copy(coded.at[k], got_coded.at[k], 0, k)

    def send_scale(k):
        return pair.copy(scale.at[k], got_scale.at[k], 1, k)

    def send_rest():
        rest = pl.ds(lead, chunks - lead)
        return pair.copy(scale.at[rest], got_scale.at[rest], 1, lead)

    def begin(k, carry):
        load(k, params_hbm, mine, load_sem.at[0, k]).start()
        load(k, public_hbm, shared, load_sem.at[1, k]).start()
        return carry

    lax.fori_loop(0, chunks, begin, 0)

    if last:

        @pl.when(pair.upper == 1)
        def _():
            pl.semaphore_wait(barrier, 1)
            pair.tell(ready)

    def encode(k, carry):
        rows, first = place(k, cols)
        load(k, params_hbm, mine, load_sem.at[0, k]).wait()
        load(k, public_hbm, shared, load_sem.at[1, k]).wait()
        for strip in range(0, WIDE, STRIP):
            columns = pl.ds(pl.multiple_of(first + strip, STRIP), STRIP)
            difference = mine[rows, columns] - shared[rows, columns]
            peak = jnp.max(jnp.abs(difference), axis=0, keepdims=True) + 1e-06
            rounded = peak.astype(jnp.bfloat16)
            scale[k, :, strip : strip + STRIP] = rounded
            wide = rounded.astype(jnp.float32)
            level = jnp.floor(difference / wide * 127.0 + 0.5)
            coded[k, :, strip : strip + STRIP] = level.astype(jnp.bfloat16)
        for strip in range(0, WIDE, STRIP):
            columns = pl.ds(pl.multiple_of(first + strip, STRIP), STRIP)
            factor = scale[k, :, strip : strip + STRIP].astype(jnp.float32) * (1.0 / 127.0)
            level = coded[k, :, strip : strip + STRIP].astype(jnp.float32)
            shared[rows, columns] = shared[rows, columns] + level * factor

        @pl.when(k == 0)
        def _():
            if last:

                @pl.when(pair.upper == 0)
                def _():
                    pl.semaphore_wait(ready, 1)
            else:
                pl.semaphore_wait(barrier, 1)

        @pl.when(k < lead)
        def _():
            send_scale(k).start()
            send_coded(k).start()

        load(k, peer_hbm, peer, peer_sem.at[k]).start()
        return carry

    lax.fori_loop(0, chunks, encode, 0)

    if lead < chunks:
        send_rest().start()

        def send_more(k, carry):
            send_coded(k).start()
            return carry

        lax.fori_loop(lead, stop, send_more, 0)

    if last:
        greet_pairs(pair, rows_in.shape[0], barrier)

    def combine(k, total):
        load(k, peer_hbm, peer, peer_sem.at[k]).wait()
        if last:

            @pl.when(k == chunks - 1)
            def _():
                hear_pairs(pair, rows_in.shape[0], barrier, all_in)

        @pl.when(k < lead)
        def _():
            send_scale(k).wait_recv()

        if lead < chunks:

            @pl.when(k == lead)
            def _():
                send_rest().wait_recv()

        send_coded(k).wait_recv()
        return merge(
            pair, k, k, total, got_coded, got_scale, mine, shared, peer, mine, peer,
            lambda rows, columns, strip: (rows, columns),
        )

    part[...] = lax.fori_loop(0, stop, combine, jnp.zeros((1, STRIP), jnp.float32))

    def drain(k, carry):
        send_coded(k).wait_send()

        @pl.when(k < lead)
        def _():
            send_scale(k).wait_send()

        return carry

    def drain_all():
        lax.fori_loop(0, stop, drain, 0)
        if lead < chunks:
            send_rest().wait_send()

    if last:
        total = add_rows(pair, part, rows_in, row_send, row_recv, all_in)
        drain_all()
        gap_out[...] = jnp.broadcast_to(total * inverse, gap_out.shape)
    else:

        def land(k, carry):
            load(k, peer_hbm, peer, peer_sem.at[k]).wait()
            return carry

        lax.fori_loop(stop, chunks, land, 0)
        scale_out[...] = got_scale[...]
        drain_all()


def last_kernel(bit, inverse, mine, shared, peer, coded, got_scale, part_in, *refs):
    mine_new, peer_new, gap_out, got_coded, send_sem, recv_sem = refs[:6]
    ready, all_in, part, rows_in, row_send, row_recv = refs[6:]
    chunks = coded.shape[0]
    start = cut(chunks)
    pair = Pair(bit, send_sem, recv_sem)
    n = rows_in.shape[0]
    barrier = pltpu.get_barrier_semaphore()

    @pl.when(pair.upper == 0)
    def _():
        pair.tell(barrier)

    @pl.when(pair.upper == 1)
    def _():
        pl.semaphore_wait(barrier, 1)
        pair.tell(ready)

    @pl.when(pair.upper == 0)
    def _():
        pl.semaphore_wait(ready, 1)

    def send_coded(k):
        return pair.copy(coded.at[k], got_coded.at[k - start], 0, k)

    def send(k, carry):
        send_coded(k).start()
        return carry

    lax.fori_loop(start, chunks, send, 0)
    greet_pairs(pair, n, barrier)

    @pl.when(start == chunks)
    def _():
        hear_pairs(pair, n, barrier, all_in)

    def combine(k, total):
        @pl.when(k == chunks - 1)
        def _():
            hear_pairs(pair, n, barrier, all_in)

        send_coded(k).wait_recv()
        slot = k - start
        return merge(
            pair, k, slot, total, got_coded, got_scale, mine, shared, peer, mine_new, peer_new,
            lambda rows, columns, strip: (slot, slice(None), slice(strip, strip + STRIP)),
        )

    part[...] = lax.fori_loop(start, chunks, combine, part_in[...])
    total = add_rows(pair, part, rows_in, row_send, row_recv, all_in)

    def drain(k, carry):
        send_coded(k).wait_send()
        return carry

    lax.fori_loop(start, chunks, drain, 0)
    gap_out[...] = jnp.broadcast_to(total * inverse, gap_out.shape)


def whole_store_kernel(*refs):
    sources, gap, targets, sem, one = refs[:3], refs[3], refs[4:8], refs[8], refs[9]
    one[...] = gap[:, :1]
    pairs = zip((one, *sources), (targets[3], *targets[:3]))
    copies = [pltpu.make_async_copy(a, b, sem.at[i]) for i, (a, b) in enumerate(pairs)]
    for copy in copies:
        copy.start()
    for copy in copies:
        copy.wait()


def early_store_kernel(chunks, mine, shared, peer, part, mine_hbm, shared_hbm, peer_hbm, part_out, sem, shared_sem):
    stop = cut(chunks)
    cols = shared.shape[1]

    def copies(k):
        here = area(k, cols)
        return [
            pltpu.make_async_copy(a.at[here], b.at[here], sem.at[i, k])
            for i, (a, b) in enumerate(((mine, mine_hbm), (peer, peer_hbm)))
        ]

    whole = pltpu.make_async_copy(shared, shared_hbm, shared_sem)
    whole.start()

    def start(k, carry):
        for copy in copies(k):
            copy.start()
        return carry

    def wait(k, carry):
        for copy in copies(k):
            copy.wait()
        return carry

    lax.fori_loop(0, stop, start, 0)
    part_out[...] = part[...]
    whole.wait()
    lax.fori_loop(0, stop, wait, 0)


def late_store_kernel(chunks, mine, peer, gap, mine_old, peer_old, mine_hbm, peer_hbm, gap_hbm, sem, gap_sem, one):
    first = cut(chunks)
    cols = mine_hbm.shape[1]

    def copies(k):
        here = area(k, cols)
        return [
            pltpu.make_async_copy(a.at[k - first], b.at[here], sem.at[i, k])
            for i, (a, b) in enumerate(((mine, mine_hbm), (peer, peer_hbm)))
        ]

    one[...] = gap[:, :1]
    small = pltpu.make_async_copy(one, gap_hbm, gap_sem)
    small.start()

    def start(k, carry):
        for copy in copies(k):
            copy.start()
        return carry

    def wait(k, carry):
        for copy in copies(k):
            copy.wait()
        return carry

    lax.fori_loop(first, chunks, start, 0)
    small.wait()
    lax.fori_loop(first, chunks, wait, 0)


def shape(*dims):
    return pltpu.HBM(dims, jnp.float32)


def params_of(limit, collective_id=None):
    if collective_id is None:
        return pltpu.CompilerParams(vmem_limit_bytes=limit)
    return pltpu.CompilerParams(
        collective_id=collective_id, has_side_effects=True, vmem_limit_bytes=limit
    )


def cost(array, passes):
    return pl.CostEstimate(flops=passes * array.size, bytes_accessed=passes * array.size, transcendentals=0)


def row_scratch(n):
    return [
        pltpu.SemaphoreType.REGULAR,
        pltpu.SemaphoreType.REGULAR,
        pltpu.VMEM((1, STRIP), jnp.float32),
        pltpu.VMEM((n, 1, STRIP), jnp.float32),
        pltpu.SemaphoreType.DMA,
        pltpu.SemaphoreType.DMA,
    ]


def open_round(bit, last, params, public, peer_public):
    rows, cols = params.shape
    chunks = rows // BLOCK * (cols // WIDE)
    n = lax.axis_size("node")
    lead = chunks if last else min(2, chunks)
    full = pltpu.VMEM(params.shape, jnp.float32)
    levels = (chunks, BLOCK, WIDE)
    scales = (chunks, 1, WIDE)
    sems = [pltpu.SemaphoreType.DMA((2, chunks))] + [pltpu.SemaphoreType.DMA((chunks,))]
    sems += [pltpu.SemaphoreType.DMA((2, chunks))] * 2
    out = [full, full, full]
    scratch = [pltpu.VMEM(levels, jnp.bfloat16), pltpu.VMEM(scales, jnp.bfloat16), pltpu.VMEM(scales, jnp.bfloat16)]
    if last:
        out += [pltpu.VMEM((1, STRIP), jnp.float32)]
        scratch = [pltpu.VMEM(levels, jnp.bfloat16)] + scratch + sems + row_scratch(n)
    else:
        out += [pltpu.VMEM(levels, jnp.bfloat16), pltpu.VMEM(scales, jnp.bfloat16), pltpu.VMEM((1, STRIP), jnp.float32)]
        scratch = scratch + sems
    return pl.pallas_call(
        partial(first_kernel, bit, lead, last, 1.0 / (n * rows * cols)),
        in_specs=[ANY] * 3,
        out_specs=[VMEM] * len(out),
        out_shape=out,
        scratch_shapes=scratch,
        cost_estimate=cost(params, 30),
        compiler_params=params_of(24 << 20, 2 * bit + 1),
    )(params, public, peer_public)


def close_round(bit, chunks, *arrays):
    rows, cols = arrays[0].shape
    n = lax.axis_size("node")
    rest = chunks - min(chunks * f // 16 for f in FIRST)
    tail = pltpu.VMEM((rest, BLOCK, WIDE), jnp.float32)
    return pl.pallas_call(
        partial(last_kernel, bit, 1.0 / (n * rows * cols)),
        in_specs=[VMEM] * 6,
        out_specs=[VMEM] * 3,
        out_shape=[tail, tail, pltpu.VMEM((1, STRIP), jnp.float32)],
        scratch_shapes=[
            pltpu.VMEM((rest, BLOCK, WIDE), jnp.bfloat16),
            pltpu.SemaphoreType.DMA((1, chunks)),
            pltpu.SemaphoreType.DMA((1, chunks)),
        ]
        + row_scratch(n),
        cost_estimate=cost(arrays[0], 10),
        compiler_params=params_of(8 << 20, 2 * bit + 2),
    )(*arrays)


def store_all(*arrays):
    return pl.pallas_call(
        whole_store_kernel,
        in_specs=[VMEM] * 4,
        out_specs=[HBM] * 4,
        out_shape=[shape(*a.shape) for a in arrays[:3]] + [shape(1, 1)],
        scratch_shapes=[pltpu.SemaphoreType.DMA((4,)), pltpu.VMEM((1, 1), jnp.float32)],
        compiler_params=params_of(1 << 20),
    )(*arrays)


def store_early(chunks, mine, shared, peer, part):
    return pl.pallas_call(
        partial(early_store_kernel, chunks),
        in_specs=[VMEM] * 4,
        out_specs=[HBM] * 3 + [VMEM],
        out_shape=[shape(*mine.shape)] * 3 + [pltpu.VMEM(part.shape, jnp.float32)],
        scratch_shapes=[pltpu.SemaphoreType.DMA((2, chunks)), pltpu.SemaphoreType.DMA],
        compiler_params=params_of(1 << 20),
    )(mine, shared, peer, part)


def store_late(chunks, mine, peer, gap, mine_hbm, peer_hbm):
    return pl.pallas_call(
        partial(late_store_kernel, chunks),
        in_specs=[VMEM] * 3 + [HBM] * 2,
        out_specs=[HBM] * 3,
        out_shape=[shape(*mine_hbm.shape)] * 2 + [shape(1, 1)],
        input_output_aliases={3: 0, 4: 1},
        scratch_shapes=[
            pltpu.SemaphoreType.DMA((2, chunks)),
            pltpu.SemaphoreType.DMA,
            pltpu.VMEM((1, 1), jnp.float32),
        ],
        compiler_params=params_of(1 << 20),
    )(mine, peer, gap, mine_hbm, peer_hbm)


def round_of(bit, params, public, peer_public):
    if bit == 0:
        return store_all(*open_round(bit, True, params, public, peer_public))
    mine, shared, peer, coded, scale, part = open_round(bit, False, params, public, peer_public)
    chunks = coded.shape[0]
    params_new, public_new, peer_new, part = store_early(chunks, mine, shared, peer, part)
    mine, peer, gap = close_round(bit, chunks, mine, shared, peer, coded, scale, part)
    params_new, peer_new, gap = store_late(chunks, mine, peer, gap, params_new, peer_new)
    return params_new, public_new, peer_new, gap


def shards(params, public, peer_public, round_index):
    n = lax.axis_size("node")
    bit_count = n.bit_length() - 1
    chosen_bit = lax.rem(round_index[0], jnp.int32(bit_count))
    branches = [partial(round_of, bit) for bit in range(bit_count)]
    params_new, public_new, peer_new, gap = lax.switch(
        chosen_bit, branches, params, public, peer_public
    )
    return (params_new, public_new, peer_new, gap[0, 0])


def solution(mesh):
    in_specs = (P("node", None), P("node", None), P("node", None), P())
    out_specs = (P("node", None), P("node", None), P("node", None), P())
    return jax.shard_map(shards, mesh=mesh, in_specs=in_specs, out_specs=out_specs, check_vma=False)
```

time: 67.1 us -> 61.1 us (0.911)
  Pallas kernels: 64.3 us -> 59.7 us
  between operations: 2.46 us -> 1.29 us
    pallas_call x2 -> x4, Pallas kernels: 64.3 us -> 59.7 us  [the longest x1 30.3 us: open_round(): pl.pallas_call(partial(first_kernel, bit, lead, last, 1.0 / (n * rows * c...]
where the time goes in v1:
time: 61.1 us; the launch traced here: 61 us
  Pallas kernels  59.7 us (98%)
  between operations  1.29 us (2%)
    pallas_call x1, Pallas kernels, open_round(): pl.pallas_call(partial(first_kernel, bit, lead, last, 1.0 / (n * rows * c...  30.3 us
    pallas_call x1, Pallas kernels, close_round(): pl.pallas_call(partial(last_kernel, bit, 1.0 / (n * rows * cols)), in_spe...  23.5 us
    pallas_call x1, Pallas kernels, store_early(): pl.pallas_call(partial(early_store_kernel, chunks), in_specs=[VMEM] * 4,...  3.56 us
    pallas_call x1, Pallas kernels, store_late(): pl.pallas_call(partial(late_store_kernel, chunks), in_specs=[VMEM] * 3 +...  2.31 us

profile of v1, /device:TPU:0, one launch (start us, length us, event | category | flops | bytes accessed | tf_op | source)
XLA Modules:
  0.0 61.0 jit_solution(16957382641759434082)
XLA Ops:
  1.3 59.7 %conditional.1 = (f32[512,2048]{1,0:T(8,128)}, f32[512,2048]{1,0:T(8,128)}, f32[512,2048]{1,0:T(8,128)}, f32[]{:T(128)}) conditional(s32[]{:T(128)} %bitcast.5, (f32[512,2048]{1,0:T(8,128)}, f32[512,2048]{1,0:T(8,128)}, f32[512,2048]{1,0:T(8,128)}) %tuple.32, (f32[512,2048]{1,0:T(8,128)}, f32[512,2048]{1,0:T(8,128)}, ...), branch_computations={%region_0.0_spmd, %region_1.0_spmd, %region_2.0_spmd, %region_3.0_... | conditional | flops 41943040 | bytes 41943072 | solution.py:544
  1.3 30.3 %branch_3_fun.4 = (f32[512,2048]{1,0:T(8,128)S(1)}, f32[512,2048]{1,0:T(8,128)S(1)}, f32[512,2048]{1,0:T(8,128)S(1)}, bf16[16,128,512]{2,1,0:T(8,128)(2,1)S(1)},...) custom-call(f32[512,2048]{1,0:T(8,128)} %get-tuple-element.84.params_hbm, ...), custom_call_target="tpu_custom_call" | custom-call | flops 31457280 | bytes 31457280 | tf_op jit(solution)/shard_map/cond/branch_3_fun/pallas_call | solution.py:458
  31.6 3.6 %branch_3_fun.5 = (f32[512,2048]{1,0:T(8,128)}, f32[512,2048]{1,0:T(8,128)}, f32[512,2048]{1,0:T(8,128)}, f32[1,128]{1,0:T(1,128)S(1)}) custom-call(f32[512,2048]{1,0:T(8,128)S(1)} %get-tuple-element.87.mine, f32[512,2048]{1,0:T(8,128)S(1)} %get-tuple-element.88.shared, f32[512,2048]{1,0:T(8,128)S(1)} %get-tuple-element.89.peer, ...), custom_call_target="tpu_custom_call" | custom-call | tf_op jit(solution)/shard_map/cond/branch_3_fun/pallas_call | solution.py:502
  35.2 23.5 %branch_3_fun.6 = (f32[8,128,512]{2,1,0:T(8,128)S(1)}, f32[8,128,512]{2,1,0:T(8,128)S(1)}, f32[1,128]{1,0:T(1,128)S(1)}) custom-call(f32[512,2048]{1,0:T(8,128)S(1)} %get-tuple-element.87.mine, f32[512,2048]{1,0:T(8,128)S(1)} %get-tuple-element.88.shared, f32[512,2048]{1,0:T(8,128)S(1)} %get-tuple-element.89.peer, ...), custom_call_target="tpu_custom_call" | custom-call | flops 10485760 | bytes 10485760 | tf_op jit(solution)/shard_map/cond/branch_3_fun/pallas_call | solution.py:474
  58.7 2.3 %branch_3_fun.7 = (f32[512,2048]{1,0:T(8,128)}, f32[512,2048]{1,0:T(8,128)}, f32[1,1]{1,0:T(1,128)}) custom-call(f32[8,128,512]{2,1,0:T(8,128)S(1)} %get-tuple-element.94.mine, f32[8,128,512]{2,1,0:T(8,128)S(1)} %get-tuple-element.95.peer, f32[1,128]{1,0:T(1,128)S(1)} %get-tuple-element.96.gap, ...), custom_call_target="tpu_custom_call", output_to_operand_aliasing={{0}: (3, {}), {1}: (4, {})} | custom-call | tf_op jit(solution)/shard_map/cond/branch_3_fun/pallas_call | solution.py:513
